TPU v7x, 16 devices: a whole 2x2x2 slice. The times are simulated.
16 devices in a mesh: dp: 1, sp: 16 (over x, y, z, core).
Axes of the slice: x: 2, y: 2, z: 2, core: 2. Of those that a mesh axis runs over, the one named last changes fastest.
Arguments:
- q: bfloat16 [32, 64, 112], P('dp')
- k: bfloat16 [32, 4096, 64, 112], P('dp', 'sp')
- v: bfloat16 [32, 4096, 64, 112], P('dp', 'sp')
Outputs:
- q: bfloat16 [32, 64, 112], P('dp')
All inputs are finite; a program needn't handle non-finite values.
Results may differ from a plain program's by a relative error of at most 0.012.
Values are sent between devices in bfloat16 or wider.
A program may use at most 2 GiB of HBM per device.

v0:
```python
import jax
import jax.numpy as jnp
from jax import lax
from jax.sharding import PartitionSpec as P


def einsum(form, a, b):
    return jnp.einsum(form, a.astype(jnp.float32), b.astype(jnp.float32))


def part_of(q, k, v):
    grouped = q.reshape(q.shape[0], k.shape[2], -1, q.shape[2])
    scores = einsum("bgsd,bugd->bgsu", grouped, k) * q.shape[2] ** -0.5
    high = jnp.max(scores, -1, keepdims=True)
    weights = jnp.exp(scores - high)
    seen = einsum("bgsu,bugd->bgsd", weights.astype(jnp.bfloat16), v)
    return jnp.concatenate([seen, jnp.sum(weights, -1, keepdims=True), high], -1)


def together(parts):
    seen, total, high = parts[..., :-2], parts[..., -2:-1], parts[..., -1:]
    scale = jnp.exp(high - jnp.max(high, 0))
    return (jnp.sum(seen * scale, 0) / jnp.sum(total * scale, 0)).astype(jnp.bfloat16)


def solution(mesh):
    def step(q, k, v):
        return together(lax.all_gather(part_of(q, k, v), "sp")).reshape(q.shape)

    return jax.shard_map(
        step,
        mesh=mesh,
        in_specs=(P("dp", None, None), P("dp", "sp", None, None), P("dp", "sp", None, None)),
        out_specs=P("dp", None, None),
        check_vma=False,
    )
```

profile of v0, /device:TPU:0, one launch (start us, length us, event | category | flops | bytes accessed | tf_op | source)
XLA Modules:
  0.0 248.8 jit_solution(842881486738558729)
XLA Ops:
  6.5 0.0 all-gather.3.cloned.1.call-start
  6.5 38.2 %fusion.7 = f32[32,64,1,256]{3,2,1,0:T(1,128)S(1)} fusion(bf16[32,256,64,112]{1,3,2,0:T(8,128)(2,1)} %param.4, bf16[32,64,112,1]{2,1,0,3:T(8,128)(2,1)} %bitcast.24), kind=kOutput, calls=%fused_computation.12 | convolution fusion | flops 117440512 | bytes 119996416 | tf_op jit(solution)/shard_map/bgsd,bugd->bgsu/dot_general | solution.py:8
  44.7 0.3 fusion.5
  45.1 0.8 fusion.6
  45.9 43.1 %fusion.1 = f32[32,64,1,112]{3,2,1,0:T(1,128)} fusion(bf16[32,256,64,112]{1,3,2,0:T(8,128)(2,1)} %param.5, bf16[32,64,256,1]{2,1,0,3:T(8,128)(2,1)S(1)} %get-tuple-element.7), kind=kOutput, calls=%fused_computation.3 | convolution fusion | flops 117440512 | bytes 119406592 | tf_op jit(solution)/shard_map/bgsu,bugd->bgsd/dot_general | solution.py:8
  89.0 2.7 %copy.10 = f32[32,64,1,112]{1,0,3,2:T(8,128)S(1)} copy(f32[32,64,1,112]{3,2,1,0:T(1,128)} %fusion.1) | data formatting | bytes 1835008 | tf_op jit(solution)/shard_map/bgsu,bugd->bgsd/dot_general | solution.py:8
  91.7 1.5 pad_maximum_fusion
  93.1 0.0 all-gather.3.cloned.1.call-update
  93.2 133.0 %all-gather.3.cloned.1.call-done = f32[512,64,1,114]{1,0,3,2:T(8,128)} async-done(((f32[32,64,1,114]{1,0,3,2:T(8,128)}), f32[512,64,1,114]{1,0,3,2:T(8,128)}) %all-gather.3.cloned.1.call-update) | async-done | bytes 14942224 | tf_op jit(solution)/shard_map/all_gather | solution.py:28
  226.1 1.0 slice_reduce_fusion
  227.1 1.1 fusion.9
  228.2 11.8 %fusion = f32[32,64,112]{1,0,2:T(8,128)S(1)} fusion(f32[16,32,64,1,114]{2,1,0,4,3:T(8,128)} %bitcast.23, f32[16,32,64]{2,1,0:T(8,128)S(1)} %get-tuple-element.6), kind=kLoop, calls=%fused_computation.1 | loop fusion | flops 7110656 | bytes 15728640 | tf_op jit(solution)/shard_map/reduce_sum | solution.py:23
  240.0 0.2 divide_convert_fusion
  240.2 1.7 copy.6
Async XLA Ops:
  6.5 219.6 %all-gather.3.cloned.1.call-start = ((), (), s32[]{:S(2)}) async-start(), calls=%async_computation | async-start | bytes 31752192 | tf_op jit(solution)/shard_map/all_gather | solution.py:28
Sparse Core Ops, SparseCore 0:
  93.3 132.8 all-gather.2
where the time goes:
time: 249 us
  waiting for transfers between devices  133 us (53%)
  matrix products  81.3 us (33%)
  other arithmetic  16.6 us (7%)
  between operations  13.4 us (5%)
  local copies, waits for them, and re-layouts  4.41 us (2%)
    all_gather x1, waiting for transfers between devices, step(): return together(lax.all_gather(part_of(q, k, v), 'sp')).reshape(q.shape)  133 us
    dot_general x2, matrix products, einsum(): return jnp.einsum(form, a.astype(jnp.float32), b.astype(jnp.float32))  81.3 us
    reduce_sum x1, other arithmetic, together(): jnp.sum(seen * scale, 0) / jnp.sum(total * scale, 0)  11.8 us
  transfers between devices with their start and end apart: 1, of which 1 were waited for; matrix products, arithmetic and copies ran while one was open for 0% of the time, Pallas kernels for 0%

commit v1 on v0

v1 whole, which is shorter than its diff:
```python
import functools

import jax
import jax.numpy as jnp
from jax import lax
from jax.experimental import pallas as pl
from jax.experimental.pallas import tpu as pltpu
from jax.sharding import PartitionSpec as P

HIGH, TOTAL, ROW = 112, 120, 128
GROUP = 16
SLOTS = 3
SENDS = 4


def masked(x):
    shape = (x.shape[0], *x.shape)
    keep = lax.broadcasted_iota(jnp.int32, shape, 0) == lax.broadcasted_iota(jnp.int32, shape, 1)
    return jnp.where(keep, x[None], jnp.zeros((), x.dtype))


def weights_of(q, k):
    each = lax.dot_general(masked(q), k, (((2,), (1,)), ((0,), (0,))), preferred_element_type=jnp.float32)
    scores = jnp.sum(each, 0) * q.shape[1] ** -0.5
    high = jnp.max(scores, -1, keepdims=True)
    weights = jnp.exp(scores - high)
    return weights.astype(q.dtype), high, jnp.sum(weights, -1, keepdims=True)


def seen_of(weights, v):
    each = lax.dot_general(masked(weights), v, (((2,), (2,)), ((0,), (0,))), preferred_element_type=jnp.float32)
    return jnp.sum(each, 0)


def kernel(n, q_hbm, k_ref, v_ref, out_ref, q_ref, keys, values, part, got, held, q_sem, k_sem, v_sem, part_sem, got_sem, send_sem, out_sem):
    me = lax.axis_index("sp")
    batch, heads, _ = q_ref.shape
    own, groups = batch // n, heads // GROUP
    sent = batch - own
    first = lax.rem((me + 1) * own, batch)

    def rows(g):
        return pl.ds(g * GROUP, GROUP)

    def sequence(j):
        return lax.rem(first + j, batch)

    def fetch_k(j):
        slot = lax.rem(j, SLOTS)
        return pltpu.make_async_copy(k_ref.at[sequence(j)], keys.at[slot], k_sem.at[slot])

    def fetch_v(j, g):
        slot = lax.rem(j, SLOTS)
        return pltpu.make_async_copy(v_ref.at[sequence(j), rows(g)], values.at[slot, rows(g)], v_sem.at[slot, g])

    def fetch(j):
        fetch_k(j).start()
        for g in range(groups):
            fetch_v(j, g).start()

    def other(step):
        return sum(bit * lax.rem(lax.div(me, bit) + lax.div(step, bit), 2) for bit in (1, 2, 4, 8))

    def to(place):
        return dict(device_id={"sp": place}, device_id_type=pl.DeviceIdType.MESH)

    query = pltpu.make_async_copy(q_hbm, q_ref, q_sem)
    query.start()
    for j in range(SLOTS):
        fetch(j)

    barrier = pltpu.get_barrier_semaphore()

    @pl.loop(1, n)
    def _(step):
        pl.semaphore_signal(barrier, inc=1, **to(other(step)))

    pl.semaphore_wait(barrier, n - 1)
    query.wait()

    lane = lax.broadcasted_iota(jnp.int32, (heads, ROW), 1)
    for u in range(own):
        got[u, me] = jnp.where((lane >= HIGH) & (lane < TOTAL), jnp.finfo(jnp.float32).min, 0.0)

    def send_part(j):
        slot, b = lax.rem(j, SENDS), sequence(j)
        u = lax.rem(b, own)
        return pltpu.make_async_remote_copy(part.at[slot], got.at[u, me], part_sem.at[slot], got_sem.at[u, me], **to(lax.div(b, own)))

    @pl.loop(0, sent)
    def _(j):
        slot, b, turn = lax.rem(j, SLOTS), sequence(j), lax.rem(j, SENDS)
        fetch_k(j).wait()
        for g in range(groups):
            fetch_v(j, g).wait()

        @pl.when(j >= SENDS)
        def _():
            send_part(j - SENDS).wait_send()

        for g in range(groups):
            at = rows(g)
            weights, high, total = weights_of(q_ref[b, at], keys[slot, at])
            part[turn, at, :HIGH] = seen_of(weights, values[slot, at])
            part[turn, at, HIGH:TOTAL] = jnp.broadcast_to(high, (GROUP, TOTAL - HIGH))
            part[turn, at, TOTAL:] = jnp.broadcast_to(total, (GROUP, ROW - TOTAL))
        send_part(j).start()

        @pl.when(j + SLOTS < batch)
        def _():
            fetch(j + SLOTS)

    def send_out(u, g, step):
        at = out_ref.at[me * own + u, rows(g)]
        return pltpu.make_async_remote_copy(at, at, send_sem.at[u, g, step], out_sem.at[u, g, me], **to(other(step)))

    @pl.loop(0, own)
    def _(u):
        j = sent + u
        slot, b = lax.rem(j, SLOTS), sequence(j)

        @pl.loop(1, n)
        def _(step):
            at = got.at[u, other(step)]
            pltpu.make_async_copy(at, at, got_sem.at[u, other(step)]).wait()

        for g in range(groups):
            parts = got[u, :, rows(g)]
            high = jnp.max(parts[:, :, HIGH:HIGH + 1], 0)
            put = jnp.sum(parts * jnp.exp(parts[:, :, HIGH:HIGH + 1] - high[None]), 0)
            held[0, rows(g)] = put
            held[1, rows(g)] = jnp.broadcast_to(high, (GROUP, ROW))

        fetch_k(j).wait()
        mine = [weights_of(q_ref[b, rows(g)], keys[slot, rows(g)]) for g in range(groups)]
        for g in range(groups):
            weights, high, total = mine[g]
            fetch_v(j, g).wait()
            seen = seen_of(weights, values[slot, rows(g)])
            theirs = held[1, rows(g), :1]
            both = jnp.maximum(theirs, high)
            old, new = jnp.exp(theirs - both), jnp.exp(high - both)
            put = held[0, rows(g)] * old
            out_ref[b, rows(g)] = ((put[:, :HIGH] + seen * new) / (put[:, TOTAL:TOTAL + 1] + total * new)).astype(out_ref.dtype)

            @pl.loop(1, n)
            def _(step):
                send_out(u, g, n - step).start()

    @pl.loop(sent - SENDS, sent)
    def _(j):
        send_part(j).wait_send()

    @pl.loop(0, own)
    def _(u):
        @pl.loop(0, groups)
        def _(g):
            @pl.loop(1, n)
            def _(step):
                send_out(u, g, step).wait_send()
                place = other(step)
                at = out_ref.at[place * own + u, rows(g)]
                pltpu.make_async_copy(at, at, out_sem.at[u, g, place]).wait()


def solution(mesh):
    n = mesh.shape["sp"]

    def step(q, k, v):
        batch, keys, heads, head = k.shape
        own, groups = batch // n, heads // GROUP
        return pl.pallas_call(
            functools.partial(kernel, n),
            out_shape=jax.ShapeDtypeStruct(q.shape, q.dtype),
            in_specs=[pl.BlockSpec(memory_space=pl.ANY)] * 3,
            out_specs=pl.BlockSpec(memory_space=pltpu.VMEM),
            scratch_shapes=[
                pltpu.VMEM(q.shape, q.dtype),
                pltpu.VMEM((SLOTS, heads, head, keys), k.dtype),
                pltpu.VMEM((SLOTS, heads, head, keys), v.dtype),
                pltpu.VMEM((SENDS, heads, ROW), jnp.float32),
                pltpu.VMEM((own, n, heads, ROW), jnp.float32),
                pltpu.VMEM((2, heads, ROW), jnp.float32),
                pltpu.SemaphoreType.DMA,
                pltpu.SemaphoreType.DMA((SLOTS,)),
                pltpu.SemaphoreType.DMA((SLOTS, groups)),
                pltpu.SemaphoreType.DMA((SENDS,)),
                pltpu.SemaphoreType.DMA((own, n)),
                pltpu.SemaphoreType.DMA((own, groups, n)),
                pltpu.SemaphoreType.DMA((own, groups, n)),
            ],
            compiler_params=pltpu.CompilerParams(collective_id=0, has_side_effects=True, vmem_limit_bytes=60 * 2**20),
        )(q, jnp.transpose(k, (0, 2, 3, 1)), jnp.transpose(v, (0, 2, 3, 1)))

    return jax.shard_map(
        step,
        mesh=mesh,
        in_specs=(P("dp", None, None), P("dp", "sp", None, None), P("dp", "sp", None, None)),
        out_specs=P("dp", None, None),
        check_vma=False,
    )
```

time: 249 us -> 101 us (0.41)
  waiting for transfers between devices: 133 us -> 0 us
  Pallas kernels: 0 us -> 98.8 us
  matrix products: 81.3 us -> 0 us
  other arithmetic: 16.6 us -> 0 us
  between operations: 13.4 us -> 0.01 us
  local copies, waits for them, and re-layouts: 4.41 us -> 1.87 us
    all_gather x1 -> x0, waiting for transfers between devices: 133 us -> none  [step(): return together(lax.all_gather(part_of(q, k, v), 'sp')).reshape(q.shape)]
    pallas_call x0 -> x1, Pallas kernels: none -> 98.8 us  [step(): pl.pallas_call(functools.partial(kernel, n), out_shape=jax.ShapeDtypeStru...]
    dot_general x2 -> x0, matrix products: 81.3 us -> none  [einsum(): return jnp.einsum(form, a.astype(jnp.float32), b.astype(jnp.float32))]
    reduce_sum x2 -> x0, other arithmetic: 12.9 us -> none  [the longest x1 11.8 us: together(): jnp.sum(seen * scale, 0) / jnp.sum(total * scale, 0)]
    dot_general x1 -> x0, local copies, waits for them, and re-layouts: 2.67 us -> none  [einsum(): return jnp.einsum(form, a.astype(jnp.float32), b.astype(jnp.float32))]
  transfers between devices with their start and end apart: 1 -> 0, of which waited for: 1 -> 0; matrix products, arithmetic and copies ran while one was open for 0% -> 0% of each run, Pallas kernels for 0% -> 0%
where the time goes in v1:
time: 101 us
  Pallas kernels  98.8 us (98%)
  local copies, waits for them, and re-layouts  1.87 us (2%)
    pallas_call x1, Pallas kernels, step(): pl.pallas_call(functools.partial(kernel, n), out_shape=jax.ShapeDtypeStru...  98.8 us

profile of v1, /device:TPU:0, one launch (start us, length us, event | category | flops | bytes accessed | tf_op | source)
XLA Modules:
  0.0 100.6 jit_solution(6516872700817879393)
XLA Ops:
  0.0 98.8 %shard_map.37 = bf16[32,64,112]{2,1,0:T(8,128)(2,1)} custom-call(bf16[32,64,112]{2,1,0:T(8,128)(2,1)} %q_hbm.1, bf16[32,64,112,256]{3,2,1,0:T(8,128)(2,1)} %bitcast.k_ref, bf16[32,64,112,256]{3,2,1,0:T(8,128)(2,1)} %bitcast.1.v_ref), custom_call_target="tpu_custom_call" | custom-call | tf_op jit(solution)/shard_map/pallas_call | solution.py:172
  98.8 1.9 %copy.5 = bf16[32,64,112]{2,1,0:T(8,128)(2,1)} copy(bf16[32,64,112]{2,1,0:T(8,128)(2,1)} %shard_map.37) | data formatting | bytes 917504

commit v2 on v0

v2 whole, which is shorter than its diff:
```python
import functools

import jax
import jax.numpy as jnp
from jax import lax
from jax.experimental import pallas as pl
from jax.experimental.pallas import tpu as pltpu
from jax.sharding import PartitionSpec as P

HIGH, TOTAL, ROW = 112, 120, 128
GROUP = 16
STEP = 32
SLOTS = 6
SENDS = 4


def alone(x, h):
    return jnp.where(lax.broadcasted_iota(jnp.int32, (x.shape[0], 1), 0) == h, x, jnp.zeros((), x.dtype))


def over_heads(x, other, contract):
    each = [lax.dot_general(alone(x, h), other(h), ((contract[:1], contract[1:]), ((), ())), preferred_element_type=jnp.float32) for h in range(GROUP)]
    even = lax.rem(lax.broadcasted_iota(jnp.int32, (GROUP, 1), 0), 2) == 0
    return jnp.where(even, sum(each[2::2], each[0]), sum(each[3::2], each[1]))


def weights_of(q, k):
    scores = over_heads(q, k, (1, 0)) * q.shape[1] ** -0.5
    high = jnp.max(scores, -1, keepdims=True)
    weights = jnp.exp(scores - high)
    return weights.astype(q.dtype), high, jnp.sum(weights, -1, keepdims=True)


def kernel(n, q_hbm, k_ref, v_ref, out_ref, q_ref, keys, values, part, got, held, q_sem, k_sem, v_sem, part_sem, got_sem, send_sem, out_sem):
    me = lax.axis_index("sp")
    batch, heads, _ = q_ref.shape
    own, halves, groups = batch // n, heads // STEP, STEP // GROUP
    rounds = own * halves
    steps = rounds * n

    def other(flip):
        return sum(bit * lax.rem(lax.div(me, bit) + lax.div(flip, bit), 2) for bit in (1, 2, 4, 8))

    def to(place):
        return dict(device_id={"sp": place}, device_id_type=pl.DeviceIdType.MESH)

    def owner(j):
        return other(n - 1 - lax.rem(j, n))

    def rows_of(place, r):
        return place * own + lax.div(r, halves), pl.multiple_of(lax.rem(r, halves) * STEP, STEP)

    def group(start, g):
        return pl.ds(pl.multiple_of(start + g * GROUP, GROUP), GROUP)

    def fetch_k(j):
        b, start = rows_of(owner(j), lax.div(j, n))
        slot = lax.rem(j, SLOTS)
        return pltpu.make_async_copy(k_ref.at[b, pl.ds(start, STEP)], keys.at[slot], k_sem.at[slot])

    def fetch_v(j, g):
        b, start = rows_of(owner(j), lax.div(j, n))
        slot = lax.rem(j, SLOTS)
        return pltpu.make_async_copy(v_ref.at[b, group(start, g)], values.at[slot, group(0, g)], v_sem.at[slot, g])

    def fetch(j):
        fetch_k(j).start()

        @pl.loop(0, groups)
        def _(g):
            fetch_v(j, g).start()

    def wait(ref, sem):
        pltpu.make_async_copy(ref, ref, sem).wait()

    query = pltpu.make_async_copy(q_hbm, q_ref, q_sem)
    query.start()

    @pl.loop(0, SLOTS)
    def _(j):
        fetch(j)

    barrier = pltpu.get_barrier_semaphore()

    @pl.loop(1, n)
    def _(flip):
        pl.semaphore_signal(barrier, inc=1, **to(other(flip)))

    pl.semaphore_wait(barrier, n - 1)
    query.wait()

    lane = lax.broadcasted_iota(jnp.int32, (STEP, ROW), 1)
    for r in range(rounds):
        got[r, me] = jnp.where((lane >= HIGH) & (lane < TOTAL), jnp.finfo(jnp.float32).min, 0.0)

    def next_fetch(j):
        @pl.when(j + SLOTS < steps)
        def _():
            fetch(j + SLOTS)

    @pl.loop(0, rounds)
    def _(r):
        @pl.loop(0, n - 1)
        def _(i):
            j = r * n + i
            place = owner(j)
            b, start = rows_of(place, r)
            slot, turn = lax.rem(j, SLOTS), lax.rem(r * (n - 1) + i, SENDS)
            fetch_k(j).wait()
            for g in range(groups):
                fetch_v(j, g).wait()

            @pl.when(r * (n - 1) + i >= SENDS)
            def _():
                wait(part.at[turn], part_sem.at[turn])

            mine = [weights_of(q_ref[b, group(start, g)], lambda h: keys[slot, g * GROUP + h]) for g in range(groups)]
            for g in range(groups):
                at = group(0, g)
                weights, high, total = mine[g]
                part[turn, at, :HIGH] = over_heads(weights, lambda h: values[slot, g * GROUP + h], (1, 1))
                part[turn, at, HIGH:TOTAL] = jnp.broadcast_to(high, (GROUP, TOTAL - HIGH))
                part[turn, at, TOTAL:] = jnp.broadcast_to(total, (GROUP, ROW - TOTAL))
            pltpu.make_async_remote_copy(part.at[turn], got.at[r, me], part_sem.at[turn], got_sem.at[r], **to(place)).start()
            next_fetch(j)

        j = r * n + n - 1
        b, start = rows_of(me, r)
        slot = lax.rem(j, SLOTS)
        fetch_k(j).wait()
        mine = [weights_of(q_ref[b, group(start, g)], lambda h: keys[slot, g * GROUP + h]) for g in range(groups)]

        wait(got.at[r, pl.ds(0, n - 1)], got_sem.at[r])
        for g in range(groups):
            parts = got[r, :, group(0, g)]
            high = jnp.max(parts[:, :, HIGH:HIGH + 1], 0)
            held[0, group(0, g)] = jnp.sum(parts * jnp.exp(parts[:, :, HIGH:HIGH + 1] - high[None]), 0)
            held[1, group(0, g)] = jnp.broadcast_to(high, (GROUP, ROW))

        for g in range(groups):
            weights, high, total = mine[g]
            fetch_v(j, g).wait()
            seen = over_heads(weights, lambda h: values[slot, g * GROUP + h], (1, 1))
            theirs = held[1, group(0, g), :1]
            both = jnp.maximum(theirs, high)
            old, new = jnp.exp(theirs - both), jnp.exp(high - both)
            put = held[0, group(0, g)] * old
            at = out_ref.at[b, group(start, g)]
            at[...] = ((put[:, :HIGH] + seen * new) / (put[:, TOTAL:TOTAL + 1] + total * new)).astype(out_ref.dtype)
            for flip in range(n - 1, 0, -1):
                pltpu.make_async_remote_copy(at, at, send_sem, out_sem, **to(other(flip))).start()
        next_fetch(j)

    for turn in range(SENDS):
        wait(part.at[turn], part_sem.at[turn])
    wait(out_ref.at[pl.ds(0, batch - own)], send_sem)
    wait(out_ref.at[pl.ds(0, batch - own)], out_sem)


def solution(mesh):
    n = mesh.shape["sp"]

    def step(q, k, v):
        batch, keys, heads, head = k.shape
        rounds, groups = batch * heads // STEP // n, STEP // GROUP
        return pl.pallas_call(
            functools.partial(kernel, n),
            out_shape=jax.ShapeDtypeStruct(q.shape, q.dtype),
            in_specs=[pl.BlockSpec(memory_space=pl.ANY)] * 3,
            out_specs=pl.BlockSpec(memory_space=pltpu.VMEM),
            scratch_shapes=[
                pltpu.VMEM(q.shape, q.dtype),
                pltpu.VMEM((SLOTS, STEP, head, keys), k.dtype),
                pltpu.VMEM((SLOTS, STEP, head, keys), v.dtype),
                pltpu.VMEM((SENDS, STEP, ROW), jnp.float32),
                pltpu.VMEM((rounds, n, STEP, ROW), jnp.float32),
                pltpu.VMEM((2, STEP, ROW), jnp.float32),
                pltpu.SemaphoreType.DMA,
                pltpu.SemaphoreType.DMA((SLOTS,)),
                pltpu.SemaphoreType.DMA((SLOTS, groups)),
                pltpu.SemaphoreType.DMA((SENDS,)),
                pltpu.SemaphoreType.DMA((rounds,)),
                pltpu.SemaphoreType.DMA,
                pltpu.SemaphoreType.DMA,
            ],
            compiler_params=pltpu.CompilerParams(collective_id=0, has_side_effects=True, vmem_limit_bytes=48 * 2**20),
        )(pltpu.with_memory_space_constraint(q, pltpu.HBM), jnp.transpose(k, (0, 2, 3, 1)), jnp.transpose(v, (0, 2, 3, 1)))

    return jax.shard_map(
        step,
        mesh=mesh,
        in_specs=(P("dp", None, None), P("dp", "sp", None, None), P("dp", "sp", None, None)),
        out_specs=P("dp", None, None),
        check_vma=False,
    )
```

time: 249 us -> 79.3 us (0.32)
  waiting for transfers between devices: 133 us -> 0 us
  matrix products: 81.3 us -> 0 us
  Pallas kernels: 0 us -> 78.4 us
  other arithmetic: 16.6 us -> 0 us
  between operations: 13.4 us -> 0.01 us
  local copies, waits for them, and re-layouts: 4.41 us -> 0.8 us
    all_gather x1 -> x0, waiting for transfers between devices: 133 us -> none  [step(): return together(lax.all_gather(part_of(q, k, v), 'sp')).reshape(q.shape)]
    dot_general x2 -> x0, matrix products: 81.3 us -> none  [einsum(): return jnp.einsum(form, a.astype(jnp.float32), b.astype(jnp.float32))]
    pallas_call x0 -> x1, Pallas kernels: none -> 78.4 us  [step(): pl.pallas_call(functools.partial(kernel, n), out_shape=jax.ShapeDtypeStru...]
    reduce_sum x2 -> x0, other arithmetic: 12.9 us -> none  [the longest x1 11.8 us: together(): jnp.sum(seen * scale, 0) / jnp.sum(total * scale, 0)]
    dot_general x1 -> x0, local copies, waits for them, and re-layouts: 2.67 us -> none  [einsum(): return jnp.einsum(form, a.astype(jnp.float32), b.astype(jnp.float32))]
  transfers between devices with their start and end apart: 1 -> 0, of which waited for: 1 -> 0; matrix products, arithmetic and copies ran while one was open for 0% -> 0% of each run, Pallas kernels for 0% -> 0%
where the time goes in v2:
time: 79.3 us; the launch traced here: 79.2 us
  Pallas kernels  78.4 us (99%)
  local copies, waits for them, and re-layouts  0.8 us (1%)
    pallas_call x1, Pallas kernels, step(): pl.pallas_call(functools.partial(kernel, n), out_shape=jax.ShapeDtypeStru...  78.4 us

profile of v2, /device:TPU:0, one launch (start us, length us, event | category | flops | bytes accessed | tf_op | source)
XLA Modules:
  0.0 79.2 jit_solution(716758210696221800)
XLA Ops:
  0.0 78.4 %shard_map.37 = bf16[32,64,112]{2,1,0:T(8,128)(2,1)S(1)} custom-call(bf16[32,64,112]{2,1,0:T(8,128)(2,1)} %q_hbm.1, bf16[32,64,112,256]{3,2,1,0:T(8,128)(2,1)} %bitcast.k_ref, bf16[32,64,112,256]{3,2,1,0:T(8,128)(2,1)} %bitcast.1.v_ref), custom_call_target="tpu_custom_call" | custom-call | tf_op jit(solution)/shard_map/pallas_call | solution.py:166
  78.4 0.8 %copy.5 = bf16[32,64,112]{2,1,0:T(8,128)(2,1)} copy(bf16[32,64,112]{2,1,0:T(8,128)(2,1)S(1)} %shard_map.37) | data formatting | bytes 917504

commit v3 on v2

v3 whole, which is shorter than its diff:
```python
import functools

import jax
import jax.numpy as jnp
from jax import lax
from jax.experimental import pallas as pl
from jax.experimental.pallas import tpu as pltpu
from jax.sharding import PartitionSpec as P

HIGH, TOTAL, ROW = 112, 120, 128
GROUP = 16
STEP = 32
SLOTS = 6
SENDS = 4


def alone(x, h):
    return jnp.where(lax.broadcasted_iota(jnp.int32, (x.shape[0], 1), 0) == h, x, jnp.zeros((), x.dtype))


def over_heads(x, other, contract):
    each = [lax.dot_general(alone(x, h), other(h), ((contract[:1], contract[1:]), ((), ())), preferred_element_type=jnp.float32) for h in range(GROUP)]
    even = lax.rem(lax.broadcasted_iota(jnp.int32, (GROUP, 1), 0), 2) == 0
    return jnp.where(even, sum(each[2::2], each[0]), sum(each[3::2], each[1]))


def weights_of(q, k):
    scores = over_heads(q, k, (1, 0)) * q.shape[1] ** -0.5
    high = jnp.max(scores, -1, keepdims=True)
    weights = jnp.exp(scores - high)
    return weights.astype(q.dtype), high, jnp.sum(weights, -1, keepdims=True)


def kernel(n, q_hbm, k_ref, v_ref, out_ref, q_ref, keys, values, part, got, kept, kept_high, kept_total, q_sem, k_sem, v_sem, part_sem, got_sem, send_sem, out_sem):
    me = lax.axis_index("sp")
    batch, heads, _ = q_ref.shape
    rounds, halves, groups = batch // n, heads // STEP, STEP // GROUP
    turns = n * halves
    steps = rounds * turns

    def other(flip):
        return sum(bit * lax.rem(lax.div(me, bit) + lax.div(flip, bit), 2) for bit in (1, 2, 4, 8))

    def to(place):
        return dict(device_id={"sp": place}, device_id_type=pl.DeviceIdType.MESH)

    def owner(j):
        return other(n - 1 - lax.div(lax.rem(j, turns), halves))

    def rows_of(j):
        return owner(j) * rounds + lax.div(j, turns), pl.multiple_of(lax.rem(j, halves) * STEP, STEP)

    def group(start, g):
        return pl.ds(pl.multiple_of(start + g * GROUP, GROUP), GROUP)

    def fetch_k(j):
        b, start = rows_of(j)
        slot = lax.rem(j, SLOTS)
        return pltpu.make_async_copy(k_ref.at[b, pl.ds(start, STEP)], keys.at[slot], k_sem.at[slot])

    def value_copy(j, g):
        b, start = rows_of(j)
        slot = lax.rem(j, SLOTS)
        return pltpu.make_async_copy(v_ref.at[b, group(start, g)], values.at[slot, group(0, g)], v_sem.at[slot, g])

    def fetch_v(j):
        @pl.loop(0, groups)
        def _(g):
            value_copy(j, g).start()

    def wait(ref, sem):
        pltpu.make_async_copy(ref, ref, sem).wait()

    query = pltpu.make_async_copy(q_hbm, q_ref, q_sem)
    query.start()

    fetch_k(0).start()

    @pl.loop(1, SLOTS)
    def _(j):
        fetch_k(j).start()
        fetch_v(j - 1)

    fetch_v(SLOTS - 1)

    barrier = pltpu.get_barrier_semaphore()

    @pl.loop(1, n)
    def _(flip):
        pl.semaphore_signal(barrier, inc=1, **to(other(flip)))

    pl.semaphore_wait(barrier, n - 1)
    query.wait()

    def weigh(j):
        b, start = rows_of(j)
        slot, turn = lax.rem(j, SLOTS), lax.rem(j, 2)
        for g in range(groups):
            weights, high, total = weights_of(q_ref[b, group(start, g)], lambda h: keys[slot, g * GROUP + h])
            kept[turn, group(0, g)] = weights
            kept_high[turn, group(0, g)] = jnp.broadcast_to(high, (GROUP, ROW))
            kept_total[turn, group(0, g)] = jnp.broadcast_to(total, (GROUP, ROW))

    def seen_of(j, g):
        slot, turn = lax.rem(j, SLOTS), lax.rem(j, 2)
        return over_heads(kept[turn, group(0, g)], lambda h: values[slot, g * GROUP + h], (1, 1))

    def next_fetch(j):
        @pl.when(j + 1 + SLOTS < steps)
        def _():
            fetch_k(j + 1 + SLOTS).start()

        @pl.when(j + SLOTS < steps)
        def _():
            fetch_v(j + SLOTS)

    def send_out(rows, flip):
        pltpu.make_async_remote_copy(rows, rows, send_sem, out_sem, **to(other(flip))).start()

    hops = {flip: (flip // 2).bit_count() for flip in range(1, n)}
    far = [flip for flip in sorted(hops, key=lambda flip: (-hops[flip], -(flip // 2), flip % 2)) if hops[flip] > 1]
    close = [flip for flip in range(n - 1, 0, -1) if hops[flip] < 2]

    fetch_k(0).wait()
    weigh(0)
    fetch_k(SLOTS).start()

    @pl.loop(0, rounds)
    def _(r):
        @pl.loop(0, turns - halves)
        def _(i):
            j, sent = r * turns + i, r * (turns - halves) + i
            place, half = owner(j), lax.rem(i, halves)
            turn, to_send = lax.rem(j, 2), lax.rem(sent, SENDS)
            fetch_k(j + 1).wait()
            for g in range(groups):
                value_copy(j, g).wait()

            @pl.when(sent >= SENDS)
            def _():
                wait(part.at[to_send], part_sem.at[to_send])

            weigh(j + 1)
            for g in range(groups):
                at = group(0, g)
                part[to_send, at, :HIGH] = seen_of(j, g)
                part[to_send, at, HIGH:TOTAL] = kept_high[turn, at, HIGH:TOTAL]
                part[to_send, at, TOTAL:] = kept_total[turn, at, TOTAL:]
            near = lax.div(i, halves * (n - 2))
            pltpu.make_async_remote_copy(part.at[to_send], got.at[r, half, me], part_sem.at[to_send], got_sem.at[r, half, near], **to(place)).start()
            next_fetch(j)

        for half in range(halves):
            j = (r + 1) * turns - halves + half
            b, start = rows_of(j)
            turn, last = lax.rem(j, 2), half == halves - 1
            seen = []
            if last:
                for g in range(groups - 1):
                    value_copy(j, g).wait()
                    seen.append(seen_of(j, g))
            else:
                fetch_k(j + 1).wait()
            for g in range(len(seen), groups):
                value_copy(j, g).wait()
            wait(got.at[r, half, pl.ds(0, n - 2)], got_sem.at[r, half, 0])
            wait(got.at[r, half, other(1)], got_sem.at[r, half, 1])
            if not last:
                weigh(j + 1)
            seen += [seen_of(j, g) for g in range(len(seen), groups)]
            for g in range(groups):
                parts = [got[r, half, other(flip), group(0, g)] for flip in range(1, n)]
                high = kept_high[turn, group(0, g), :1]
                top = functools.reduce(jnp.maximum, [x[:, HIGH:HIGH + 1] for x in parts], high)
                new = jnp.exp(high - top)
                rest = sum(x * jnp.exp(x[:, HIGH:HIGH + 1] - top) for x in parts)
                total = rest[:, TOTAL:TOTAL + 1] + kept_total[turn, group(0, g), :1] * new
                at = out_ref.at[b, group(start, g)]
                at[...] = (rest[:, :HIGH] / total + seen[g] * (new / total)).astype(out_ref.dtype)
            for flip in far:
                send_out(out_ref.at[b, pl.ds(start, STEP)], flip)
            if last:
                for flip in close:
                    send_out(out_ref.at[b], flip)

                @pl.when(j + 1 < steps)
                def _():
                    fetch_k(j + 1).wait()
                    weigh(j + 1)
            next_fetch(j)

    for turn in range(SENDS):
        wait(part.at[turn], part_sem.at[turn])
    wait(out_ref.at[pl.ds(0, batch - rounds)], send_sem)
    wait(out_ref.at[pl.ds(0, batch - rounds)], out_sem)


def solution(mesh):
    n = mesh.shape["sp"]

    def step(q, k, v):
        batch, keys, heads, head = k.shape
        rounds, halves, groups = batch // n, heads // STEP, STEP // GROUP
        return pl.pallas_call(
            functools.partial(kernel, n),
            out_shape=jax.ShapeDtypeStruct(q.shape, q.dtype),
            in_specs=[pl.BlockSpec(memory_space=pl.ANY)] * 3,
            out_specs=pl.BlockSpec(memory_space=pltpu.VMEM),
            scratch_shapes=[
                pltpu.VMEM(q.shape, q.dtype),
                pltpu.VMEM((SLOTS, STEP, head, keys), k.dtype),
                pltpu.VMEM((SLOTS, STEP, head, keys), v.dtype),
                pltpu.VMEM((SENDS, STEP, ROW), jnp.float32),
                pltpu.VMEM((rounds, halves, n, STEP, ROW), jnp.float32),
                pltpu.VMEM((2, STEP, keys), q.dtype),
                pltpu.VMEM((2, STEP, ROW), jnp.float32),
                pltpu.VMEM((2, STEP, ROW), jnp.float32),
                pltpu.SemaphoreType.DMA,
                pltpu.SemaphoreType.DMA((SLOTS,)),
                pltpu.SemaphoreType.DMA((SLOTS, groups)),
                pltpu.SemaphoreType.DMA((SENDS,)),
                pltpu.SemaphoreType.DMA((rounds, halves, 2)),
                pltpu.SemaphoreType.DMA,
                pltpu.SemaphoreType.DMA,
            ],
            compiler_params=pltpu.CompilerParams(collective_id=0, has_side_effects=True, vmem_limit_bytes=48 * 2**20),
        )(pltpu.with_memory_space_constraint(q, pltpu.HBM), jnp.transpose(k, (0, 2, 3, 1)), jnp.transpose(v, (0, 2, 3, 1)))

    return jax.shard_map(
        step,
        mesh=mesh,
        in_specs=(P("dp", None, None), P("dp", "sp", None, None), P("dp", "sp", None, None)),
        out_specs=P("dp", None, None),
        check_vma=False,
    )
```

time: 79.3 us -> 78.7 us (level)
  no operation moved by 1% of the time
where the time goes in v3:
time: 78.7 us; the launch traced here: 78.6 us
  Pallas kernels  77.7 us (99%)
  local copies, waits for them, and re-layouts  0.8 us (1%)
    pallas_call x1, Pallas kernels, step(): pl.pallas_call(functools.partial(kernel, n), out_shape=jax.ShapeDtypeStru...  77.7 us

profile of v3, /device:TPU:0, one launch (start us, length us, event | category | flops | bytes accessed | tf_op | source)
XLA Modules:
  0.0 78.6 jit_solution(14013964239050284504)
XLA Ops:
  0.0 77.7 %shard_map.37 = bf16[32,64,112]{2,1,0:T(8,128)(2,1)S(1)} custom-call(bf16[32,64,112]{2,1,0:T(8,128)(2,1)} %q_hbm.1, bf16[32,64,112,256]{3,2,1,0:T(8,128)(2,1)} %bitcast.k_ref, bf16[32,64,112,256]{3,2,1,0:T(8,128)(2,1)} %bitcast.1.v_ref), custom_call_target="tpu_custom_call" | custom-call | tf_op jit(solution)/shard_map/pallas_call | solution.py:204
  77.8 0.8 %copy.5 = bf16[32,64,112]{2,1,0:T(8,128)(2,1)} copy(bf16[32,64,112]{2,1,0:T(8,128)(2,1)S(1)} %shard_map.37) | data formatting | bytes 917504

commit v4 on v3

--- a/solution.py
+++ b/solution.py
@@ -10,8 +10,9 @@
 HIGH, TOTAL, ROW = 112, 120, 128
 GROUP = 16
 STEP = 32
-SLOTS = 6
+SLOTS = 8
 SENDS = 4
+AHEAD = 2
 
 
 def alone(x, h):
@@ -74,14 +75,18 @@
     query = pltpu.make_async_copy(q_hbm, q_ref, q_sem)
     query.start()
 
-    fetch_k(0).start()
-
-    @pl.loop(1, SLOTS)
+    @pl.loop(0, AHEAD)
     def _(j):
         fetch_k(j).start()
-        fetch_v(j - 1)
-
-    fetch_v(SLOTS - 1)
+
+    @pl.loop(AHEAD, SLOTS)
+    def _(j):
+        fetch_k(j).start()
+        fetch_v(j - AHEAD)
+
+    @pl.loop(SLOTS - AHEAD, SLOTS)
+    def _(j):
+        fetch_v(j)
 
     barrier = pltpu.get_barrier_semaphore()
 
@@ -94,7 +99,7 @@
 
     def weigh(j):
         b, start = rows_of(j)
-        slot, turn = lax.rem(j, SLOTS), lax.rem(j, 2)
+        slot, turn = lax.rem(j, SLOTS), lax.rem(j, AHEAD + 1)
         for g in range(groups):
             weights, high, total = weights_of(q_ref[b, group(start, g)], lambda h: keys[slot, g * GROUP + h])
             kept[turn, group(0, g)] = weights
@@ -102,13 +107,13 @@
             kept_total[turn, group(0, g)] = jnp.broadcast_to(total, (GROUP, ROW))
 
     def seen_of(j, g):
-        slot, turn = lax.rem(j, SLOTS), lax.rem(j, 2)
+        slot, turn = lax.rem(j, SLOTS), lax.rem(j, AHEAD + 1)
         return over_heads(kept[turn, group(0, g)], lambda h: values[slot, g * GROUP + h], (1, 1))
 
     def next_fetch(j):
-        @pl.when(j + 1 + SLOTS < steps)
+        @pl.when(j + AHEAD + SLOTS < steps)
         def _():
-            fetch_k(j + 1 + SLOTS).start()
+            fetch_k(j + AHEAD + SLOTS).start()
 
         @pl.when(j + SLOTS < steps)
         def _():
@@ -121,9 +126,11 @@
     far = [flip for flip in sorted(hops, key=lambda flip: (-hops[flip], -(flip // 2), flip % 2)) if hops[flip] > 1]
     close = [flip for flip in range(n - 1, 0, -1) if hops[flip] < 2]
 
-    fetch_k(0).wait()
-    weigh(0)
-    fetch_k(SLOTS).start()
+    @pl.loop(0, AHEAD)
+    def _(j):
+        fetch_k(j).wait()
+        weigh(j)
+        fetch_k(j + SLOTS).start()
 
     @pl.loop(0, rounds)
     def _(r):
@@ -131,8 +138,8 @@
         def _(i):
             j, sent = r * turns + i, r * (turns - halves) + i
             place, half = owner(j), lax.rem(i, halves)
-            turn, to_send = lax.rem(j, 2), lax.rem(sent, SENDS)
-            fetch_k(j + 1).wait()
+            turn, to_send = lax.rem(j, AHEAD + 1), lax.rem(sent, SENDS)
+            fetch_k(j + AHEAD).wait()
             for g in range(groups):
                 value_copy(j, g).wait()
 
@@ -140,7 +147,7 @@
             def _():
                 wait(part.at[to_send], part_sem.at[to_send])
 
-            weigh(j + 1)
+            weigh(j + AHEAD)
             for g in range(groups):
                 at = group(0, g)
                 part[to_send, at, :HIGH] = seen_of(j, g)
@@ -153,20 +160,16 @@
         for half in range(halves):
             j = (r + 1) * turns - halves + half
             b, start = rows_of(j)
-            turn, last = lax.rem(j, 2), half == halves - 1
+            turn, last = lax.rem(j, AHEAD + 1), half == halves - 1
             seen = []
             if last:
                 for g in range(groups - 1):
                     value_copy(j, g).wait()
                     seen.append(seen_of(j, g))
-            else:
-                fetch_k(j + 1).wait()
             for g in range(len(seen), groups):
                 value_copy(j, g).wait()
             wait(got.at[r, half, pl.ds(0, n - 2)], got_sem.at[r, half, 0])
             wait(got.at[r, half, other(1)], got_sem.at[r, half, 1])
-            if not last:
-                weigh(j + 1)
             seen += [seen_of(j, g) for g in range(len(seen), groups)]
             for g in range(groups):
                 parts = [got[r, half, other(flip), group(0, g)] for flip in range(1, n)]
@@ -183,10 +186,11 @@
                 for flip in close:
                     send_out(out_ref.at[b], flip)
 
-                @pl.when(j + 1 < steps)
-                def _():
-                    fetch_k(j + 1).wait()
-                    weigh(j + 1)
+            @pl.when(j + AHEAD < steps)
+            def _():
+                fetch_k(j + AHEAD).wait()
+                weigh(j + AHEAD)
+
             next_fetch(j)
 
     for turn in range(SENDS):
@@ -212,9 +216,9 @@
                 pltpu.VMEM((SLOTS, STEP, head, keys), v.dtype),
                 pltpu.VMEM((SENDS, STEP, ROW), jnp.float32),
                 pltpu.VMEM((rounds, halves, n, STEP, ROW), jnp.float32),
-                pltpu.VMEM((2, STEP, keys), q.dtype),
-                pltpu.VMEM((2, STEP, ROW), jnp.float32),
-                pltpu.VMEM((2, STEP, ROW), jnp.float32),
+                pltpu.VMEM((AHEAD + 1, STEP, keys), q.dtype),
+                pltpu.VMEM((AHEAD + 1, STEP, ROW), jnp.float32),
+                pltpu.VMEM((AHEAD + 1, STEP, ROW), jnp.float32),
                 pltpu.SemaphoreType.DMA,
                 pltpu.SemaphoreType.DMA((SLOTS,)),
                 pltpu.SemaphoreType.DMA((SLOTS, groups)),

time: 78.7 us -> 78.7 us (level)
  no operation moved by 1% of the time
where the time goes in v4:
time: 78.7 us; the launch traced here: 78.6 us
  Pallas kernels  77.8 us (99%)
  local copies, waits for them, and re-layouts  0.8 us (1%)
    pallas_call x1, Pallas kernels, step(): pl.pallas_call(functools.partial(kernel, n), out_shape=jax.ShapeDtypeStru...  77.8 us

profile of v4, /device:TPU:0, one launch (start us, length us, event | category | flops | bytes accessed | tf_op | source)
XLA Modules:
  0.0 78.6 jit_solution(4953626964027211371)
XLA Ops:
  0.0 77.8 %shard_map.37 = bf16[32,64,112]{2,1,0:T(8,128)(2,1)S(1)} custom-call(bf16[32,64,112]{2,1,0:T(8,128)(2,1)} %q_hbm.1, bf16[32,64,112,256]{3,2,1,0:T(8,128)(2,1)} %bitcast.k_ref, bf16[32,64,112,256]{3,2,1,0:T(8,128)(2,1)} %bitcast.1.v_ref), custom_call_target="tpu_custom_call" | custom-call | tf_op jit(solution)/shard_map/pallas_call | solution.py:208
  77.8 0.8 %copy.5 = bf16[32,64,112]{2,1,0:T(8,128)(2,1)} copy(bf16[32,64,112]{2,1,0:T(8,128)(2,1)S(1)} %shard_map.37) | data formatting | bytes 917504
